TPU v7x, 32 devices: a whole 2x2x4 slice. The times are simulated.
32 devices in a mesh: fsdp: 4 (over x, core), vocab: 8 (over z, y).
Axes of the slice: x: 2, y: 2, z: 4, core: 2. Of those that a mesh axis runs over, the one named last changes fastest.
Arguments:
- hidden_states: bfloat16 [512, 3072], P('fsdp', 'vocab'), may hold values from -512 to 512
- head: bfloat16 [3072, 16384], P('fsdp', 'vocab'), may hold values from -0.25259074 to 0.25259074
- labels: int32 [512], P('fsdp'), may hold values from 0 to 16383
Outputs:
- token_loss: float32 [512], P('fsdp')
- state_grad: bfloat16 [512, 3072], P('fsdp', 'vocab')
- head_grad: float32 [3072, 16384], P('fsdp', 'vocab')
All inputs are finite; a program needn't handle non-finite values.
Results may differ from a plain program's by a relative error of at most 0.0034.
Values may be sent and summed in bfloat16 or wider, within the bound.
A program may use at most 128 MiB of HBM per device.

v0:
```python
import jax
import jax.numpy as jnp
from jax import lax
from jax.sharding import PartitionSpec as P


def local(hidden_states, head, labels):
    features = lax.all_gather(hidden_states, "vocab", axis=1, tiled=True)
    weights = lax.all_gather(head, "fsdp", axis=0, tiled=True)
    logits = jnp.dot(features, weights, preferred_element_type=jnp.float32)
    width = weights.shape[1]
    columns = lax.axis_index("vocab") * width + jnp.arange(width, dtype=jnp.int32)
    hits = labels[:, None] == columns[None, :]
    local_target = jnp.sum(jnp.where(hits, logits, jnp.float32(0.0)), axis=1)
    local_peak = jnp.max(logits, axis=1)
    peak = lax.pmax(local_peak, "vocab")
    shifted = jnp.exp(logits - peak[:, None])
    total, target = lax.psum((jnp.sum(shifted, axis=1), local_target), "vocab")
    token_loss = jnp.log(total) + peak - target
    errors = (shifted / total[:, None] - hits.astype(jnp.float32)).astype(jnp.bfloat16)
    state_terms = lax.dot_general(
        errors, weights, (((1,), (1,)), ((), ())), preferred_element_type=jnp.float32
    )
    state_grad = lax.psum_scatter(state_terms, "vocab", scatter_dimension=1, tiled=True).astype(
        jnp.bfloat16
    )
    all_errors = lax.all_gather(errors, "fsdp", axis=0, tiled=True)
    slices = lax.all_to_all(features, "fsdp", split_axis=1, concat_axis=0, tiled=True)
    head_grad = lax.dot_general(
        slices, all_errors, (((0,), (0,)), ((), ())), preferred_element_type=jnp.float32
    )
    return (token_loss, state_grad, head_grad)


def solution(mesh):
    in_specs = (P("fsdp", "vocab"), P("fsdp", "vocab"), P("fsdp"))
    out_specs = (P("fsdp"), P("fsdp", "vocab"), P("fsdp", "vocab"))
    return jax.shard_map(local, mesh=mesh, in_specs=in_specs, out_specs=out_specs, check_vma=False)
```

profile of v0, /device:TPU:3, one launch (start us, length us, event | category | flops | bytes accessed | tf_op | source)
XLA Modules:
  0.0 241.4 jit_solution(18237512961004457685)
XLA Ops:
  7.2 0.0 all-gather.3.cloned.1.call-start
  7.2 0.7 all-gather.3.cloned.1.call-update
  7.9 0.0 all-gather.5.cloned.1.call-start
  7.9 1.0 copy.8
  9.0 27.2 %all_gather.9 = bf16[128,3072]{0,1:T(8,128)(2,1)S(1)} all-gather(bf16[128,384]{0,1:T(8,128)(2,1)S(1)} %copy.8), channel_id=1, replica_groups=mesh['fsdp'=4,'vocab'=8] {'vocab'}, dimensions={1}, use_global_device_ids=true | all-gather | bytes 884736 | tf_op jit(solution)/shard_map/all_gather | solution.py:8
  36.2 0.0 copy-start
  36.2 56.0 %all-gather.3.cloned.1.call-done = bf16[3072,2048]{1,0:T(8,128)(2,1)} async-done(((bf16[768,2048]{1,0:T(8,128)(2,1)}), bf16[3072,2048]{1,0:T(8,128)(2,1)}) %all-gather.3.cloned.1.call-update) | async-done | bytes 12582928 | tf_op jit(solution)/shard_map/all_gather | solution.py:9
  92.2 6.5 %fusion.4 = (f32[128]{0:T(128)S(1)}, f32[128,2048]{1,0:T(8,128)S(1)}) fusion(bf16[128,3072]{0,1:T(8,128)(2,1)S(1)} %all_gather.9, bf16[3072,2048]{1,0:T(8,128)(2,1)} %all-gather.3.cloned.1.call-done), kind=kOutput, calls=%fused_computation.10 | convolution fusion | flops 1610874752 | bytes 14418432 | tf_op jit(solution)/shard_map/dot_general | solution.py:10
  98.6 17.8 %pmax.7 = f32[128]{0:T(128)S(1)} all-reduce(f32[128]{0:T(128)S(1)} %get-tuple-element.16), channel_id=1, replica_groups=mesh['fsdp'=4,'vocab'=8] {'vocab'}, use_global_device_ids=true, to_apply=%region_1.2 | all-reduce | flops 128 | bytes 1024 | tf_op jit(solution)/shard_map/pmax | solution.py:16
  116.4 0.0 copy-done
  116.4 0.4 fusion.3
  116.8 13.7 %all-reduce = (f32[128]{0:T(128)S(1)}, f32[128]{0:T(128)S(1)}) all-reduce(f32[128]{0:T(128)S(1)} %get-tuple-element.13, f32[128]{0:T(128)S(1)} %get-tuple-element.12), channel_id=1, replica_groups=mesh['fsdp'=4,'vocab'=8] {'vocab'}, use_global_device_ids=true, to_apply=%region_5.6 | all-reduce | flops 256 | bytes 2048 | tf_op jit(solution)/shard_map/psum | solution.py:18
  130.5 1.2 fusion.2
  131.7 0.0 all-gather.5.cloned.1.call-update
  131.7 0.0 reduce-scatter.2.cloned.1.call-start
  131.7 10.2 %fusion.5 = f32[128,3072]{1,0:T(8,128)} fusion(bf16[128,2048]{1,0:T(8,128)(2,1)} %fusion.2, bf16[3072,2048]{1,0:T(8,128)(2,1)} %all-gather.3.cloned.1.call-done), kind=kOutput, calls=%fused_computation.11 | convolution fusion | flops 1610612736 | bytes 14680064 | tf_op jit(solution)/shard_map/dot_general | solution.py:21
  141.9 0.0 reduce-scatter.2.cloned.1.call-update
  141.9 24.0 %all_to_all.19 = bf16[128,4,768]{0,2,1:T(8,128)(2,1)S(1)} all-to-all(bf16[128,4,768]{0,2,1:T(8,128)(2,1)S(1)} %bitcast.11), channel_id=1, replica_groups=mesh['fsdp'=4,'vocab'=8] {'fsdp'}, dimensions={1} | all-to-all | bytes 1572864 | tf_op jit(solution)/shard_map/all_to_all | solution.py:28
  165.9 0.3 copy.9
  166.2 0.5 add_subtract_fusion
  166.7 0.0 all-gather.5.cloned.1.call-done
  166.7 6.1 %convolution_bitcast_fusion = f32[768,2048]{0,1:T(8,128)} fusion(bf16[512,2048]{1,0:T(8,128)(2,1)} %all-gather.5.cloned.1.call-done, bf16[512,768]{1,0:T(8,128)(2,1)S(1)} %bitcast.12), kind=kOutput, calls=%fused_computation | convolution fusion | flops 1610612736 | bytes 9175040 | tf_op jit(solution)/shard_map/dot_general | solution.py:29
  172.8 6.6 %copy.10 = f32[768,2048]{1,0:T(8,128)} copy(f32[768,2048]{0,1:T(8,128)} %convolution_bitcast_fusion) | data formatting | bytes 12582912
  179.4 53.9 %reduce-scatter.2.cloned.1.call-done = f32[128,384]{1,0:T(8,128)} async-done(((f32[128,3072]{1,0:T(8,128)}), f32[128,384]{1,0:T(8,128)}) %reduce-scatter.2.cloned.1.call-update) | async-done | bytes 196624 | tf_op jit(solution)/shard_map/reduce_scatter | solution.py:24
  233.3 1.6 convert_element_type.11
  (1 shorter events, 0.0 us)
Async XLA Ops:
  7.2 85.0 %all-gather.3.cloned.1.call-start = ((), (), s32[]{:S(2)}) async-start(), calls=%async_computation.2 | async-start | bytes 15728640 | tf_op jit(solution)/shard_map/all_gather | solution.py:9
  7.9 158.8 %all-gather.5.cloned.1.call-start = ((), (), s32[]{:S(2)}) async-start(), calls=%async_computation.4 | async-start | bytes 2621440 | tf_op jit(solution)/shard_map/all_gather | solution.py:27
  36.2 80.3 %copy-start = (s32[128]{0:T(128)S(1)}, s32[128]{0:T(128)}, u32[]{:S(2)}) copy-start(s32[128]{0:T(128)} %param.5) | copy-start | bytes 1540
  131.7 101.6 %reduce-scatter.2.cloned.1.call-start = ((), (), s32[]{:S(2)}) async-start(), calls=%async_computation.3 | async-start | bytes 1769472 | tf_op jit(solution)/shard_map/reduce_scatter | solution.py:24
Sparse Core Ops, SparseCore 0:
  9.5 82.5 all-gather.2
  131.8 30.1 all-gather.4
  165.4 67.8 reduce-scatter.1
where the time goes:
time: 245 us; the launch traced here: 241 us
  waiting for transfers between devices  111 us (45%)
  blocking collectives  82.7 us (34%)
  matrix products  22.7 us (9%)
  between operations  13.8 us (6%)
  local copies, waits for them, and re-layouts  7.85 us (3%)
  other arithmetic  3.66 us (1%)
    all_gather x1, waiting for transfers between devices, local(): weights = lax.all_gather(head, 'fsdp', axis=0, tiled=True)  56 us
    reduce_scatter x1, waiting for transfers between devices, local(): lax.psum_scatter(state_terms, 'vocab', scatter_dimension=1, tiled=True)  53.9 us
    all_gather x1, blocking collectives, local(): features = lax.all_gather(hidden_states, 'vocab', axis=1, tiled=True)  27.2 us
    all_to_all x1, blocking collectives, local(): lax.all_to_all(features, 'fsdp', split_axis=1, concat_axis=0, tiled=True)  24 us
    pmax x1, blocking collectives, local(): peak = lax.pmax(local_peak, 'vocab')  17.8 us
    psum x1, blocking collectives, local(): total, target = lax.psum((jnp.sum(shifted, axis=1), local_target), 'vocab')  13.7 us
    dot_general x1, matrix products, local(): lax.dot_general(errors, weights, (((1,), (1,)), ((), ())), preferred_elem...  10.2 us
    unnamed x4, local copies, waits for them, and re-layouts  7.57 us
  transfers between devices with their start and end apart: 3, of which 2 were waited for; matrix products, arithmetic and copies ran while one was open for 10% of the time, Pallas kernels for 0%

commit v1 on v0

v1 whole, which is shorter than its diff:
```python
import functools

import jax
import jax.numpy as jnp
from jax import lax
from jax.experimental import pallas as pl
from jax.experimental.pallas import tpu as pltpu
from jax.sharding import PartitionSpec as P

CORES = 2
MESH = pl.DeviceIdType.MESH
NT = (((1,), (1,)), ((), ()))


def tile_of(size):
    return 256 if size % 256 == 0 else 128


def kernel(nf, nv, x_ref, head_hbm, lab_ref, loss_ref, grad_ref, err_out, feat_out,
           head, first, feats, labs, part, sib, xrecv, stats, errs, stf, stb, recv2, outb, fin,
           loc_sem, f1_s, f1_r, f2_s, f2_r, lab_s, lab_r, d_s, d_r, x_s, x_r, t_s, t_r,
           e_s, e_r, g_s, g_r, q_s, q_r, o_s, o_r):
    f = lax.axis_index("fsdp")
    v = lax.axis_index("vocab")
    r = nv // nf
    nx = nf // CORES
    xi, c = f // CORES, lax.rem(f, CORES)
    other = f + 1 - 2 * c
    width = head.shape[1]
    half = width // CORES
    tokens = feats.shape[0]
    tc = tokens // nv
    tx = tokens // nx
    db = x_ref.shape[1]
    dl = feats.shape[1]

    def rcopy(src, dst, s, q, ff, vv):
        return pltpu.make_async_remote_copy(
            src_ref=src, dst_ref=dst, send_sem=s, recv_sem=q,
            device_id=(ff, vv), device_id_type=MESH)

    def rows(index, size):
        return pl.ds(pl.multiple_of(index * size, size), size)

    load = pltpu.make_async_copy(head_hbm, head, loc_sem.at[0])
    load.start()

    jm = lax.rem(v, r)
    for i in range(r):
        piece = x_ref.at[pl.ds(i * tc, tc)]
        tf, tv = v // r, r * f + i
        mine = (tf == f) & (tv == v)

        @pl.when(mine)
        def _():
            pltpu.make_async_copy(piece, first.at[jm], f1_r.at[jm]).start()

        @pl.when(jnp.logical_not(mine))
        def _():
            rcopy(piece, first.at[jm], f1_s.at[i], f1_r.at[jm], tf, tv).start()

    labcopy = rcopy(lab_ref, labs.at[c], lab_s, lab_r, other, v)
    labcopy.start()
    labs[c] = lab_ref[...]

    for j in range(r):
        pltpu.make_async_copy(first.at[j], first.at[j], f1_r.at[j]).wait()
    for j in range(r):
        feats[rows(v, tc), j * db:(j + 1) * db] = first[j]
    gathers = []
    for d in range(1, nv):
        tv = lax.rem(v + d, nv)
        cp = rcopy(feats.at[rows(v, tc)], feats.at[rows(v, tc)], f2_s.at[d], f2_r.at[d], f, tv)
        cp.start()
        gathers.append(cp)
    load.wait()
    for d in range(1, nv):
        sv = lax.rem(v + nv - d, nv)
        pltpu.make_async_copy(feats.at[rows(sv, tc)], feats.at[rows(sv, tc)], f2_r.at[d]).wait()

    nt = tile_of(half)

    def logits_half(h):
        def tile(t, carry):
            col = pl.multiple_of(h * half + t * nt, nt)
            out = pl.multiple_of(t * nt, nt)
            part[h, :, pl.ds(out, nt)] = jnp.dot(
                feats[...], head[:, pl.ds(col, nt)], preferred_element_type=jnp.float32)
            return carry
        lax.fori_loop(0, half // nt, tile, 0)

    logits_half(1 - c)
    for d in list(range(1, nx)) + [0]:
        g = lax.rem(xi + d, nx)
        rcopy(part.at[1 - c, rows(g, tx)], sib.at[rows(g, tx)], d_s.at[d], d_r.at[d], other, v).start()
    logits_half(c)
    for d in list(range(1, nx)) + [0]:
        g = lax.rem(xi + d, nx)
        pltpu.make_async_copy(sib.at[rows(g, tx)], sib.at[rows(g, tx)], d_r.at[d]).wait()
        part[c, rows(g, tx)] = part[c, rows(g, tx)] + sib[rows(g, tx)]
        if d:
            rcopy(part.at[c, rows(g, tx)], xrecv.at[d - 1], x_s.at[d], x_r.at[d], g * CORES + c, v).start()

    outfeat = pltpu.make_async_copy(feats, feat_out, loc_sem.at[1])
    outfeat.start()

    labcopy.wait_recv()
    row = jnp.concatenate([labs[k] for k in range(CORES)], axis=1).astype(jnp.float32)
    want = jnp.broadcast_to(row, (128, tx)).T[:, :1]
    iota = lax.broadcasted_iota(jnp.int32, (tx, half), 1).astype(jnp.float32)
    base = (v * width + c * half).astype(jnp.float32)
    hits = (iota + base) == want

    for d in range(1, nx):
        pltpu.make_async_copy(xrecv.at[d - 1], xrecv.at[d - 1], x_r.at[d]).wait()
    logits = part[c, rows(xi, tx)]
    for d in range(1, nx):
        logits = logits + xrecv[d - 1]
    m = jnp.max(logits, axis=1, keepdims=True)
    shifted = jnp.exp(logits - m)
    s = jnp.sum(shifted, axis=1, keepdims=True)
    tg = jnp.sum(jnp.where(hits, logits, 0.0), axis=1, keepdims=True)
    lane = lax.broadcasted_iota(jnp.int32, (tx, 128), 1)
    packed = jnp.where(lane == 0, m, jnp.where(lane == 1, s, tg))
    me = v * CORES + c
    n = nv * CORES
    stats[me] = packed.T[:8]
    for d in range(1, n):
        to = lax.rem(me + d, n)
        rcopy(stats.at[me], stats.at[me], t_s.at[d], t_r.at[d],
              xi * CORES + lax.rem(to, CORES), to // CORES).start()
    for d in range(1, n):
        fr = lax.rem(me + n - d, n)
        pltpu.make_async_copy(stats.at[fr], stats.at[fr], t_r.at[d]).wait()
    peak = stats[0, 0:1]
    for k in range(1, n):
        peak = jnp.maximum(peak, stats[k, 0:1])
    total = jnp.zeros_like(peak)
    target = jnp.zeros_like(peak)
    for k in range(n):
        total = total + stats[k, 1:2] * jnp.exp(stats[k, 0:1] - peak)
        target = target + stats[k, 2:3]
    loss = jnp.log(total) + peak - target
    size = tx // CORES
    picked = loss[:, :size]
    for k in range(1, CORES):
        picked = jnp.where(c == k, loss[:, k * size:(k + 1) * size], picked)
    loss_ref[...] = picked
    sub = lax.broadcasted_iota(jnp.int32, (128, tx), 0)
    cols = jnp.where(sub == 0, peak, total).T
    scaled = jnp.exp(logits - cols[:, 0:1]) / cols[:, 1:2]
    errs[c, rows(xi, tx)] = (scaled - hits.astype(jnp.float32)).astype(jnp.bfloat16)

    mine = errs.at[c, rows(xi, tx)]
    for d in range(1, nx):
        g = lax.rem(xi + d, nx)
        rcopy(mine, mine, e_s.at[d], e_r.at[d], g * CORES + c, v).start()
    rcopy(mine, mine, g_s.at[0], g_r.at[0], other, v).start()
    for d in range(1, nx):
        g = lax.rem(xi + nx - d, nx)
        block = errs.at[c, rows(g, tx)]
        pltpu.make_async_copy(block, block, e_r.at[d]).wait()
        rcopy(block, block, g_s.at[d], g_r.at[d], other, v).start()
    for d in range(nx):
        g = lax.rem(xi + nx - d, nx)
        block = errs.at[1 - c, rows(g, tx)]
        pltpu.make_async_copy(block, block, g_r.at[d]).wait()
    outerr = []
    for h in range(CORES):
        cp = pltpu.make_async_copy(errs.at[h], err_out.at[:, pl.ds(h * half, half)], loc_sem.at[2 + h])
        cp.start()
        outerr.append(cp)

    dt = tile_of(dl)

    def state_tile(t, carry):
        at = pl.ds(pl.multiple_of(t * dt, dt), dt)
        acc = lax.dot_general(errs[0], head[at, 0:half], NT, preferred_element_type=jnp.float32)
        for h in range(1, CORES):
            acc = acc + lax.dot_general(
                errs[h], head[at, h * half:(h + 1) * half], NT, preferred_element_type=jnp.float32)
        stf[:, at] = acc
        stb[:, at] = acc.astype(jnp.bfloat16)
        return carry

    lax.fori_loop(0, dl // dt, state_tile, 0)
    for d in range(1, nv):
        tv = lax.rem(v + d, nv)
        rcopy(stb.at[rows(tv, tc)], recv2.at[d], q_s.at[d], q_r.at[d], f, tv).start()
    acc = stf[rows(v, tc), :]
    for d in range(1, nv):
        pltpu.make_async_copy(recv2.at[d], recv2.at[d], q_r.at[d]).wait()
        acc = acc + recv2[d].astype(jnp.float32)
    final = acc.astype(jnp.bfloat16)
    for j in range(r):
        outb[j] = final[:, j * db:(j + 1) * db]
    for j in range(r):
        tf, tv = v // r, r * f + j
        own = (tf == f) & (tv == v)

        @pl.when(own)
        def _():
            pltpu.make_async_copy(outb.at[j], fin.at[jm], o_r.at[jm]).start()

        @pl.when(jnp.logical_not(own))
        def _():
            rcopy(outb.at[j], fin.at[jm], o_s.at[j], o_r.at[jm], tf, tv).start()
    for j in range(r):
        pltpu.make_async_copy(fin.at[j], fin.at[j], o_r.at[j]).wait()
        grad_ref[j * tc:(j + 1) * tc, :] = fin[j]

    for i in range(r):
        own = (v // r == f) & (r * f + i == v)

        @pl.when(jnp.logical_not(own))
        def _():
            rcopy(x_ref.at[pl.ds(i * tc, tc)], first.at[jm], f1_s.at[i], f1_r.at[jm], v // r, r * f + i).wait_send()
            rcopy(outb.at[i], fin.at[jm], o_s.at[i], o_r.at[jm], v // r, r * f + i).wait_send()

    labcopy.wait_send()
    for cp in gathers:
        cp.wait_send()
    for d in range(nx):
        g = lax.rem(xi + d, nx)
        rcopy(part.at[1 - c, rows(g, tx)], sib.at[rows(g, tx)], d_s.at[d], d_r.at[d], other, v).wait_send()
        g2 = lax.rem(xi + nx - d, nx)
        block = errs.at[c, rows(g2, tx)]
        rcopy(block, block, g_s.at[d], g_r.at[d], other, v).wait_send()
        if d:
            rcopy(part.at[c, rows(g, tx)], xrecv.at[d - 1], x_s.at[d], x_r.at[d], g * CORES + c, v).wait_send()
            rcopy(mine_block(errs, c, rows(xi, tx)), mine_block(errs, c, rows(xi, tx)),
                  e_s.at[d], e_r.at[d], g * CORES + c, v).wait_send()
    for d in range(1, n):
        to = lax.rem(me + d, n)
        rcopy(stats.at[me], stats.at[me], t_s.at[d], t_r.at[d],
              xi * CORES + lax.rem(to, CORES), to // CORES).wait_send()
    for d in range(1, nv):
        tv = lax.rem(v + d, nv)
        rcopy(stb.at[rows(tv, tc)], recv2.at[d], q_s.at[d], q_r.at[d], f, tv).wait_send()
    outfeat.wait()
    for cp in outerr:
        cp.wait()


def mine_block(errs, c, where):
    return errs.at[c, where]


def local(nf, nv, hidden_states, head, labels):
    own, db = hidden_states.shape
    dl, width = head.shape
    tokens = own * nf
    half = width // CORES
    r, nx = nv // nf, nf // CORES
    tc, tx = tokens // nv, tokens // nx
    n = nv * CORES
    f32, bf16 = jnp.float32, jnp.bfloat16
    dma = pltpu.SemaphoreType.DMA
    vmem = pl.BlockSpec(memory_space=pltpu.VMEM)
    anyw = pl.BlockSpec(memory_space=pl.ANY)
    loss, grad, errors, feats = pl.pallas_call(
        functools.partial(kernel, nf, nv),
        out_shape=(
            jax.ShapeDtypeStruct((1, own), f32),
            jax.ShapeDtypeStruct((own, db), bf16),
            jax.ShapeDtypeStruct((tokens, width), bf16),
            jax.ShapeDtypeStruct((tokens, dl), bf16),
        ),
        in_specs=[vmem, anyw, vmem],
        out_specs=(vmem, vmem, anyw, anyw),
        scratch_shapes=[
            pltpu.VMEM((dl, width), bf16),
            pltpu.VMEM((r, tc, db), bf16),
            pltpu.VMEM((tokens, dl), bf16),
            pltpu.VMEM((CORES, 1, own), jnp.int32),
            pltpu.VMEM((CORES, tokens, half), f32),
            pltpu.VMEM((tokens, half), f32),
            pltpu.VMEM((max(nx - 1, 1), tx, half), f32),
            pltpu.VMEM((n, 8, tx), f32),
            pltpu.VMEM((CORES, tokens, half), bf16),
            pltpu.VMEM((tokens, dl), f32),
            pltpu.VMEM((tokens, dl), bf16),
            pltpu.VMEM((nv, tc, dl), bf16),
            pltpu.VMEM((r, tc, db), bf16),
            pltpu.VMEM((r, tc, db), bf16),
            dma((4,)), dma((r,)), dma((r,)), dma((nv,)), dma((nv,)), dma, dma,
            dma((nx,)), dma((nx,)), dma((nx,)), dma((nx,)), dma((n,)), dma((n,)),
            dma((nx,)), dma((nx,)), dma((nx,)), dma((nx,)), dma((nv,)), dma((nv,)),
            dma((r,)), dma((r,)),
        ],
        compiler_params=pltpu.CompilerParams(has_side_effects=True, vmem_limit_bytes=60 * 1024 * 1024),
    )(hidden_states, head, labels.reshape(1, own))
    head_grad = lax.dot_general(
        feats, errors, (((0,), (0,)), ((), ())), preferred_element_type=f32)
    return (loss.reshape(own), grad, head_grad)


def solution(mesh):
    sizes = dict(mesh.shape)
    body = functools.partial(local, sizes["fsdp"], sizes["vocab"])
    in_specs = (P("fsdp", "vocab"), P("fsdp", "vocab"), P("fsdp"))
    out_specs = (P("fsdp"), P("fsdp", "vocab"), P("fsdp", "vocab"))
    return jax.shard_map(body, mesh=mesh, in_specs=in_specs, out_specs=out_specs, check_vma=False)
```

time: 245 us -> 117 us (0.48); the launches traced: 241 us -> 116 us
  waiting for transfers between devices: 111 us -> 0 us
  Pallas kernels: 0 us -> 108 us
  blocking collectives: 82.7 us -> 0 us
  matrix products: 22.7 us -> 6.41 us
  between operations: 13.8 us -> 0.66 us
  local copies, waits for them, and re-layouts: 7.85 us -> 1.16 us
  other arithmetic: 3.66 us -> 0 us
    pallas_call x0 -> x1, Pallas kernels: none -> 108 us  [local(): pl.pallas_call(functools.partial(kernel, nf, nv), out_shape=(jax.ShapeDty...]
    all_gather x2 -> x0, waiting for transfers between devices: 56 us -> none  [the longest x1 56 us: local(): weights = lax.all_gather(head, 'fsdp', axis=0, tiled=True)]
    reduce_scatter x1 -> x0, waiting for transfers between devices: 53.9 us -> none  [local(): lax.psum_scatter(state_terms, 'vocab', scatter_dimension=1, tiled=True)]
    all_gather x1 -> x0, blocking collectives: 27.2 us -> none  [local(): features = lax.all_gather(hidden_states, 'vocab', axis=1, tiled=True)]
    all_to_all x1 -> x0, blocking collectives: 24 us -> none  [local(): lax.all_to_all(features, 'fsdp', split_axis=1, concat_axis=0, tiled=True)]
    pmax x1 -> x0, blocking collectives: 17.8 us -> none  [local(): peak = lax.pmax(local_peak, 'vocab')]
    dot_general x3 -> x1, matrix products: 22.7 us -> 6.41 us  [local(): lax.dot_general(feats, errors, (((0,), (0,)), ((), ())), preferred_elemen...]
    psum x1 -> x0, blocking collectives: 13.7 us -> none  [local(): total, target = lax.psum((jnp.sum(shifted, axis=1), local_target), 'vocab')]
  transfers between devices with their start and end apart: 3 -> 0, of which waited for: 2 -> 0; matrix products, arithmetic and copies ran while one was open for 10% -> 0% of each run, Pallas kernels for 0% -> 0%
where the time goes in v1:
time: 117 us; the launch traced here: 116 us
  Pallas kernels  108 us (92%)
  matrix products  6.41 us (5%)
    pallas_call x1, Pallas kernels, local(): pl.pallas_call(functools.partial(kernel, nf, nv), out_shape=(jax.ShapeDty...  108 us
    dot_general x1, matrix products, local(): lax.dot_general(feats, errors, (((0,), (0,)), ((), ())), preferred_elemen...  6.41 us

profile of v1, /device:TPU:3, one launch (start us, length us, event | category | flops | bytes accessed | tf_op | source)
XLA Modules:
  0.0 116.4 jit_solution(10682266075766589979)
XLA Ops:
  0.6 108.1 %shard_map.58 = (f32[1,128]{1,0:T(1,128)}, bf16[128,384]{1,0:T(8,128)(2,1)}, bf16[512,2048]{1,0:T(8,128)(2,1)}, bf16[512,768]{1,0:T(8,128)(2,1)}) custom-call(bf16[128,384]{1,0:T(8,128)(2,1)} %x_ref.1, bf16[768,2048]{1,0:T(8,128)(2,1)} %head_hbm.1, s32[1,128]{1,0:T(1,128)} %bitcast.4), custom_call_target="tpu_custom_call" | custom-call | tf_op jit(solution)/shard_map/pallas_call | solution.py:261
  108.8 0.0 copy-start.1
  108.8 0.0 copy-start
  108.8 6.4 %fusion = f32[768,2048]{1,0:T(8,128)} fusion(bf16[512,768]{1,0:T(8,128)(2,1)} %get-tuple-element.9, bf16[512,2048]{1,0:T(8,128)(2,1)} %get-tuple-element.10), kind=kOutput, calls=%fused_computation | convolution fusion | flops 1610612736 | bytes 9175040 | tf_op jit(solution)/shard_map/dot_general | solution.py:293
  115.2 0.0 copy-done.1
  115.2 0.5 copy.8
  115.7 0.0 copy-done
  115.7 0.6 copy.9
Async XLA Ops:
  108.8 6.4 %copy-start.1 = (f32[1,128]{1,0:T(1,128)S(1)}, f32[1,128]{1,0:T(1,128)}, u32[]{:S(2)}) copy-start(f32[1,128]{1,0:T(1,128)} %get-tuple-element.7) | copy-start | bytes 1540
  108.8 6.9 %copy-start = (bf16[128,384]{1,0:T(8,128)(2,1)S(1)}, bf16[128,384]{1,0:T(8,128)(2,1)}, u32[]{:S(2)}) copy-start(bf16[128,384]{1,0:T(8,128)(2,1)} %get-tuple-element.15) | copy-start | bytes 294916

commit v2 on v1

--- a/solution.py
+++ b/solution.py
@@ -8,6 +8,7 @@
 from jax.sharding import PartitionSpec as P
 
 CORES = 2
+PAIR = 2
 MESH = pl.DeviceIdType.MESH
 NT = (((1,), (1,)), ((), ()))
 
@@ -67,39 +68,64 @@
         pltpu.make_async_copy(first.at[j], first.at[j], f1_r.at[j]).wait()
     for j in range(r):
         feats[rows(v, tc), j * db:(j + 1) * db] = first[j]
+    na = nv // PAIR
+    va, vb = v // PAIR, lax.rem(v, PAIR)
+    pair = v + 1 - 2 * vb
     gathers = []
-    for d in range(1, nv):
-        tv = lax.rem(v + d, nv)
+
+    def pass_on(index, d):
+        cp = rcopy(feats.at[rows(index, tc)], feats.at[rows(index, tc)],
+                   f2_s.at[na + d], f2_r.at[na + d], f, pair)
+        cp.start()
+        gathers.append(cp)
+
+    for d in range(1, na):
+        tv = lax.rem(va + d, na) * PAIR + vb
         cp = rcopy(feats.at[rows(v, tc)], feats.at[rows(v, tc)], f2_s.at[d], f2_r.at[d], f, tv)
         cp.start()
         gathers.append(cp)
+    pass_on(v, 0)
+    for d in range(1, na):
+        sv = lax.rem(va + na - d, na) * PAIR + vb
+        pltpu.make_async_copy(feats.at[rows(sv, tc)], feats.at[rows(sv, tc)], f2_r.at[d]).wait()
+        pass_on(sv, d)
     load.wait()
-    for d in range(1, nv):
-        sv = lax.rem(v + nv - d, nv)
-        pltpu.make_async_copy(feats.at[rows(sv, tc)], feats.at[rows(sv, tc)], f2_r.at[d]).wait()
+    for d in range(na):
+        sv = lax.rem(va + na - d, na) * PAIR + 1 - vb
+        pltpu.make_async_copy(feats.at[rows(sv, tc)], feats.at[rows(sv, tc)], f2_r.at[na + d]).wait()
 
     nt = tile_of(half)
 
-    def logits_half(h):
+    def logits_part(g, h):
         def tile(t, carry):
             col = pl.multiple_of(h * half + t * nt, nt)
             out = pl.multiple_of(t * nt, nt)
-            part[h, :, pl.ds(out, nt)] = jnp.dot(
-                feats[...], head[:, pl.ds(col, nt)], preferred_element_type=jnp.float32)
+            part[h, rows(g, tx), pl.ds(out, nt)] = jnp.dot(
+                feats[rows(g, tx), :], head[:, pl.ds(col, nt)], preferred_element_type=jnp.float32)
             return carry
         lax.fori_loop(0, half // nt, tile, 0)
 
-    logits_half(1 - c)
-    for d in list(range(1, nx)) + [0]:
+    def give(d):
         g = lax.rem(xi + d, nx)
         rcopy(part.at[1 - c, rows(g, tx)], sib.at[rows(g, tx)], d_s.at[d], d_r.at[d], other, v).start()
-    logits_half(c)
-    for d in list(range(1, nx)) + [0]:
+
+    def take(d):
         g = lax.rem(xi + d, nx)
         pltpu.make_async_copy(sib.at[rows(g, tx)], sib.at[rows(g, tx)], d_r.at[d]).wait()
         part[c, rows(g, tx)] = part[c, rows(g, tx)] + sib[rows(g, tx)]
         if d:
             rcopy(part.at[c, rows(g, tx)], xrecv.at[d - 1], x_s.at[d], x_r.at[d], g * CORES + c, v).start()
+
+    for d in range(1, nx):
+        logits_part(lax.rem(xi + d, nx), 1 - c)
+        give(d)
+        logits_part(lax.rem(xi + d, nx), c)
+    for d in range(1, nx):
+        take(d)
+    logits_part(xi, 1 - c)
+    give(0)
+    logits_part(xi, c)
+    take(0)
 
     outfeat = pltpu.make_async_copy(feats, feat_out, loc_sem.at[1])
     outfeat.start()

time: 117 us -> 112 us (0.957)
  Pallas kernels: 108 us -> 104 us
    pallas_call x1, Pallas kernels: 108 us -> 104 us  [local(): pl.pallas_call(functools.partial(kernel, nf, nv), out_shape=(jax.ShapeDty...]
where the time goes in v2:
time: 112 us
  Pallas kernels  104 us (93%)
  matrix products  6.4 us (6%)
  local copies, waits for them, and re-layouts  1.16 us (1%)
    pallas_call x1, Pallas kernels, local(): pl.pallas_call(functools.partial(kernel, nf, nv), out_shape=(jax.ShapeDty...  104 us
    dot_general x1, matrix products, local(): lax.dot_general(feats, errors, (((0,), (0,)), ((), ())), preferred_elemen...  6.4 us

profile of v2, /device:TPU:3, one launch (start us, length us, event | category | flops | bytes accessed | tf_op | source)
XLA Modules:
  0.0 112.3 jit_solution(14880345109019269354)
XLA Ops:
  0.6 104.1 %shard_map.58 = (f32[1,128]{1,0:T(1,128)}, bf16[128,384]{1,0:T(8,128)(2,1)}, bf16[512,2048]{1,0:T(8,128)(2,1)}, bf16[512,768]{1,0:T(8,128)(2,1)}) custom-call(bf16[128,384]{1,0:T(8,128)(2,1)} %x_ref.1, bf16[768,2048]{1,0:T(8,128)(2,1)} %head_hbm.1, s32[1,128]{1,0:T(1,128)} %bitcast.4), custom_call_target="tpu_custom_call" | custom-call | tf_op jit(solution)/shard_map/pallas_call | solution.py:287
  104.7 0.0 copy-start.1
  104.7 0.0 copy-start
  104.7 6.4 %fusion = f32[768,2048]{1,0:T(8,128)} fusion(bf16[512,768]{1,0:T(8,128)(2,1)} %get-tuple-element.9, bf16[512,2048]{1,0:T(8,128)(2,1)} %get-tuple-element.10), kind=kOutput, calls=%fused_computation | convolution fusion | flops 1610612736 | bytes 9175040 | tf_op jit(solution)/shard_map/dot_general | solution.py:319
  111.1 0.0 copy-done.1
  111.1 0.5 copy.8
  111.6 0.0 copy-done
  111.7 0.6 copy.9
Async XLA Ops:
  104.7 6.4 %copy-start.1 = (f32[1,128]{1,0:T(1,128)S(1)}, f32[1,128]{1,0:T(1,128)}, u32[]{:S(2)}) copy-start(f32[1,128]{1,0:T(1,128)} %get-tuple-element.7) | copy-start | bytes 1540
  104.7 6.9 %copy-start = (bf16[128,384]{1,0:T(8,128)(2,1)S(1)}, bf16[128,384]{1,0:T(8,128)(2,1)}, u32[]{:S(2)}) copy-start(bf16[128,384]{1,0:T(8,128)(2,1)} %get-tuple-element.15) | copy-start | bytes 294916

commit v3 on v2

--- a/solution.py
+++ b/solution.py
@@ -182,37 +182,43 @@
         g = lax.rem(xi + d, nx)
         rcopy(mine, mine, e_s.at[d], e_r.at[d], g * CORES + c, v).start()
     rcopy(mine, mine, g_s.at[0], g_r.at[0], other, v).start()
-    for d in range(1, nx):
+
+    dt = tile_of(dl)
+
+    def state_part(g):
+        def tile(t, carry):
+            at = pl.ds(pl.multiple_of(t * dt, dt), dt)
+            acc = lax.dot_general(
+                errs[0, rows(g, tx)], head[at, 0:half], NT, preferred_element_type=jnp.float32)
+            for h in range(1, CORES):
+                acc = acc + lax.dot_general(
+                    errs[h, rows(g, tx)], head[at, h * half:(h + 1) * half], NT,
+                    preferred_element_type=jnp.float32)
+            stf[rows(g, tx), at] = acc
+            stb[rows(g, tx), at] = acc.astype(jnp.bfloat16)
+            return carry
+        lax.fori_loop(0, dl // dt, tile, 0)
+        for d in range(1, nv):
+            tv = lax.rem(v + d, nv)
+
+            @pl.when(tv // (nv // nx) == g)
+            def _():
+                rcopy(stb.at[rows(tv, tc)], recv2.at[d], q_s.at[d], q_r.at[d], f, tv).start()
+
+    for d in range(nx):
         g = lax.rem(xi + nx - d, nx)
         block = errs.at[c, rows(g, tx)]
-        pltpu.make_async_copy(block, block, e_r.at[d]).wait()
-        rcopy(block, block, g_s.at[d], g_r.at[d], other, v).start()
-    for d in range(nx):
-        g = lax.rem(xi + nx - d, nx)
+        if d:
+            pltpu.make_async_copy(block, block, e_r.at[d]).wait()
+            rcopy(block, block, g_s.at[d], g_r.at[d], other, v).start()
         block = errs.at[1 - c, rows(g, tx)]
         pltpu.make_async_copy(block, block, g_r.at[d]).wait()
+        state_part(g)
     outerr = []
     for h in range(CORES):
         cp = pltpu.make_async_copy(errs.at[h], err_out.at[:, pl.ds(h * half, half)], loc_sem.at[2 + h])
         cp.start()
         outerr.append(cp)
-
-    dt = tile_of(dl)
-
-    def state_tile(t, carry):
-        at = pl.ds(pl.multiple_of(t * dt, dt), dt)
-        acc = lax.dot_general(errs[0], head[at, 0:half], NT, preferred_element_type=jnp.float32)
-        for h in range(1, CORES):
-            acc = acc + lax.dot_general(
-                errs[h], head[at, h * half:(h + 1) * half], NT, preferred_element_type=jnp.float32)
-        stf[:, at] = acc
-        stb[:, at] = acc.astype(jnp.bfloat16)
-        return carry
-
-    lax.fori_loop(0, dl // dt, state_tile, 0)
-    for d in range(1, nv):
-        tv = lax.rem(v + d, nv)
-        rcopy(stb.at[rows(tv, tc)], recv2.at[d], q_s.at[d], q_r.at[d], f, tv).start()
     acc = stf[rows(v, tc), :]
     for d in range(1, nv):
         pltpu.make_async_copy(recv2.at[d], recv2.at[d], q_r.at[d]).wait()

time: 112 us -> 112 us (level)
  no operation moved by 1% of the time
where the time goes in v3:
time: 112 us; the launch traced here: 111 us
  Pallas kernels  103 us (92%)
  matrix products  6.4 us (6%)
  local copies, waits for them, and re-layouts  1.16 us (1%)
    pallas_call x1, Pallas kernels, local(): pl.pallas_call(functools.partial(kernel, nf, nv), out_shape=(jax.ShapeDty...  103 us
    dot_general x1, matrix products, local(): lax.dot_general(feats, errors, (((0,), (0,)), ((), ())), preferred_elemen...  6.4 us

profile of v3, /device:TPU:3, one launch (start us, length us, event | category | flops | bytes accessed | tf_op | source)
XLA Modules:
  0.0 111.4 jit_solution(3152910914629290850)
XLA Ops:
  0.6 103.2 %shard_map.58 = (f32[1,128]{1,0:T(1,128)}, bf16[128,384]{1,0:T(8,128)(2,1)}, bf16[512,2048]{1,0:T(8,128)(2,1)}, bf16[512,768]{1,0:T(8,128)(2,1)}) custom-call(bf16[128,384]{1,0:T(8,128)(2,1)} %x_ref.1, bf16[768,2048]{1,0:T(8,128)(2,1)} %head_hbm.1, s32[1,128]{1,0:T(1,128)} %bitcast.4), custom_call_target="tpu_custom_call" | custom-call | tf_op jit(solution)/shard_map/pallas_call | solution.py:293
  103.9 0.0 copy-start.1
  103.9 0.0 copy-start
  103.9 6.4 %fusion = f32[768,2048]{1,0:T(8,128)} fusion(bf16[512,768]{1,0:T(8,128)(2,1)} %get-tuple-element.9, bf16[512,2048]{1,0:T(8,128)(2,1)} %get-tuple-element.10), kind=kOutput, calls=%fused_computation | convolution fusion | flops 1610612736 | bytes 9175040 | tf_op jit(solution)/shard_map/dot_general | solution.py:325
  110.3 0.0 copy-done.1
  110.3 0.5 copy.8
  110.8 0.0 copy-done
  110.8 0.6 copy.9
Async XLA Ops:
  103.9 6.4 %copy-start.1 = (f32[1,128]{1,0:T(1,128)S(1)}, f32[1,128]{1,0:T(1,128)}, u32[]{:S(2)}) copy-start(f32[1,128]{1,0:T(1,128)} %get-tuple-element.7) | copy-start | bytes 1540
  103.9 6.9 %copy-start = (bf16[128,384]{1,0:T(8,128)(2,1)S(1)}, bf16[128,384]{1,0:T(8,128)(2,1)}, u32[]{:S(2)}) copy-start(bf16[128,384]{1,0:T(8,128)(2,1)} %get-tuple-element.15) | copy-start | bytes 294916
